TPU v7x, 32 devices: a 4x2x2 block of a 4x4x8 slice. The times are simulated.
32 devices in a mesh: dp: 4 (over y, z), seq: 8 (over x, core).
Axes of the slice: x: 4, y: 2, z: 2, core: 2. Of those that a mesh axis runs over, the one named last changes fastest.
The devices are a block of a 4x4x8 slice.
Arguments:
- enc_out: bfloat16 [256, 16, 512], P('dp', 'seq'), parts along dimension 0
- pred_out: bfloat16 [256, 64, 512], P('dp'), parts along dimension 0
- w_enc: bfloat16 [512, 512], replicated
- w_pred: bfloat16 [512, 512], replicated
- w_out: bfloat16 [512, 500], replicated
- labels: int32 [256, 63], P('dp'), parts along dimension 0
- frame_len: int32 [256], P('dp'), parts along dimension 0
- label_len: int32 [256], P('dp'), parts along dimension 0
Outputs:
- output 1: float32 [256], P('dp'), parts along dimension 0
- output 2: bfloat16 [256, 16, 512], P('dp', 'seq'), parts along dimension 0
- output 3: float32 [2048, 512], P('dp'), parts along dimension 0
- output 4: float32 [2048, 512], P('dp'), parts along dimension 0
- output 5: float32 [2048, 500], P('dp'), parts along dimension 0
There are 4 independent parts. A program takes and returns all parts, laid end to end along the dimension named above; an argument that names none is the same for every part.
All inputs are finite; a program needn't handle non-finite values.
Results may differ from a plain program's by a relative error of at most 0.0142388.
Values are sent between devices in bfloat16 or wider.
A program may use at most 768 MiB of HBM per device.

v0:
```python
import jax
import jax.numpy as jnp
from jax import lax
from jax.sharding import PartitionSpec as P

NEG_FILL = -1.0e30


def label_prefix(lab_lp):
    zero_col = jnp.zeros_like(lab_lp[:, :1])
    return jnp.concatenate([zero_col, jnp.cumsum(lab_lp[:, :-1], axis=1)], axis=1)


def label_weights(labels, w_out):
    n_utt = labels.shape[0]
    lab_ids = jnp.concatenate([labels, jnp.full((n_utt, 1), -1, jnp.int32)], axis=1)
    onehot = (lab_ids[:, :, None] == lax.broadcasted_iota(jnp.int32, (1, 1, w_out.shape[1]), 2)).astype(jnp.bfloat16)
    lab_w = jnp.einsum('buv,jv->buj', onehot, w_out, preferred_element_type=jnp.float32).astype(jnp.bfloat16)
    return lab_ids, lab_w


def joint_lattice(enc_blk, act_g, lab_w, w_enc, w_out):
    act_f = jnp.einsum('bth,hj->btj', enc_blk, w_enc, preferred_element_type=jnp.float32).astype(jnp.bfloat16)
    hidden = jnp.tanh(act_f[:, :, None, :].astype(jnp.float32) + act_g[:, None, :, :].astype(jnp.float32)).astype(jnp.bfloat16)
    logits = jnp.einsum('btuj,jv->btuv', hidden, w_out, preferred_element_type=jnp.float32)
    log_norm = jax.nn.logsumexp(logits, axis=-1)
    soft_probs = jnp.exp(logits - log_norm[..., None])
    blank_lp = logits[..., 0] - log_norm
    lab_lp = jnp.einsum('btuj,buj->btu', hidden, lab_w, preferred_element_type=jnp.float32) - log_norm
    return hidden, soft_probs, blank_lp, lab_lp


def alpha_rows(x_in, blank_lp, lab_lp):
    def frame_step(x_prev, frame_in):
        frame_blank, frame_lab = frame_in
        lab_sum = label_prefix(frame_lab)
        alpha_t = lab_sum + lax.cumlogsumexp(x_prev - lab_sum, axis=1)
        return alpha_t + frame_blank, alpha_t
    x_out, alphas = lax.scan(frame_step, x_in, (jnp.swapaxes(blank_lp, 0, 1), jnp.swapaxes(lab_lp, 0, 1)))
    return x_out, jnp.swapaxes(alphas, 0, 1)


def beta_rows(next_in, blank_lp, lab_lp, frame_ids, frame_len, boundary):
    def frame_step(next_row, frame_in):
        frame_blank, frame_lab, frame_id = frame_in
        lab_sum = label_prefix(frame_lab)
        beta_row = lax.cumlogsumexp(next_row + frame_blank + lab_sum, axis=1, reverse=True) - lab_sum
        beta_row = jnp.where((frame_id >= frame_len)[:, None], boundary, beta_row)
        return beta_row, (beta_row, next_row)
    first_row, (betas, beta_next) = lax.scan(frame_step, next_in, (jnp.swapaxes(blank_lp, 0, 1), jnp.swapaxes(lab_lp, 0, 1), frame_ids), reverse=True)
    return first_row, jnp.swapaxes(betas, 0, 1), jnp.swapaxes(beta_next, 0, 1)


def occupancy(alphas, betas, beta_next, blank_lp, lab_lp, log_prob, frame_ok):
    beta_up = jnp.concatenate([betas[:, :, 1:], jnp.full_like(betas[:, :, :1], NEG_FILL)], axis=2)
    norm_shift = log_prob[:, None, None]
    occ_blank = jnp.where(frame_ok, jnp.exp(jnp.minimum(alphas + blank_lp + beta_next - norm_shift, 0.0)), 0.0)
    occ_lab = jnp.where(frame_ok, jnp.exp(jnp.minimum(alphas + lab_lp + beta_up - norm_shift, 0.0)), 0.0)
    return occ_blank, occ_lab


def joint_backward(enc_blk, hidden, soft_probs, occ_blank, occ_lab, lab_ids, w_enc, w_out):
    vocab_ids = lax.broadcasted_iota(jnp.int32, (1, 1, 1, soft_probs.shape[-1]), 3)
    d_logits = (soft_probs * (occ_blank + occ_lab)[..., None] - jnp.where(vocab_ids == 0, occ_blank[..., None], 0.0) - jnp.where(vocab_ids == lab_ids[:, None, :, None], occ_lab[..., None], 0.0)).astype(jnp.bfloat16)
    d_hidden = jnp.einsum('btuv,jv->btuj', d_logits, w_out, preferred_element_type=jnp.float32)
    d_pre = (d_hidden * (1.0 - jnp.square(hidden.astype(jnp.float32)))).astype(jnp.bfloat16)
    d_act_f = jnp.sum(d_pre, axis=2, dtype=jnp.float32).astype(jnp.bfloat16)
    d_act_g = jnp.sum(d_pre, axis=1, dtype=jnp.float32)
    grad_enc = jnp.einsum('btj,hj->bth', d_act_f, w_enc, preferred_element_type=jnp.float32).astype(jnp.bfloat16)
    gw_enc = jnp.einsum('bth,btj->hj', enc_blk, d_act_f, preferred_element_type=jnp.float32)
    gw_out = jnp.einsum('btuj,btuv->jv', hidden, d_logits, preferred_element_type=jnp.float32)
    return grad_enc, gw_enc, gw_out, d_act_g


def solution(mesh):
    seq_size = mesh.shape['seq']
    fwd_pairs = [(src, src + 1) for src in range(seq_size - 1)]
    bwd_pairs = [(src + 1, src) for src in range(seq_size - 1)]

    def local_fn(enc_out, pred_out, w_enc, w_pred, w_out, labels, frame_len, label_len):
        seq_idx = lax.axis_index('seq')
        n_utt, n_loc, _ = enc_out.shape
        lab_pos = pred_out.shape[1]
        lab_ids, lab_w = label_weights(labels, w_out)
        act_g = jnp.einsum('buh,hj->buj', pred_out, w_pred, preferred_element_type=jnp.float32).astype(jnp.bfloat16)
        hidden, soft_probs, blank_lp, lab_lp = joint_lattice(enc_out, act_g, lab_w, w_enc, w_out)
        pos_ids = lax.broadcasted_iota(jnp.int32, (n_utt, lab_pos), 1)
        neg_rows = jnp.full((n_utt, lab_pos), NEG_FILL, jnp.float32)
        init_x = jnp.where(pos_ids == 0, 0.0, neg_rows)
        boundary = jnp.where(pos_ids == label_len[:, None], 0.0, neg_rows)
        frame_ids = seq_idx * n_loc + jnp.arange(n_loc, dtype=jnp.int32)

        def alpha_hop(hop_idx, x_in):
            x_out, _ = alpha_rows(x_in, blank_lp, lab_lp)
            received = lax.ppermute(x_out, 'seq', fwd_pairs)
            return jnp.where(seq_idx == 0, init_x, received)

        x_in = lax.fori_loop(0, seq_size - 1, alpha_hop, init_x)
        _, alphas = alpha_rows(x_in, blank_lp, lab_lp)

        def beta_hop(hop_idx, next_in):
            first_row, _, _ = beta_rows(next_in, blank_lp, lab_lp, frame_ids, frame_len, boundary)
            received = lax.ppermute(first_row, 'seq', bwd_pairs)
            return jnp.where(seq_idx == seq_size - 1, boundary, received)

        next_in = lax.fori_loop(0, seq_size - 1, beta_hop, boundary)
        first_row, betas, beta_next = beta_rows(next_in, blank_lp, lab_lp, frame_ids, frame_len, boundary)
        log_prob = lax.psum(jnp.where(seq_idx == 0, first_row[:, 0], 0.0), 'seq')
        frame_ok = (frame_ids[None, :] < frame_len[:, None])[:, :, None]
        occ_blank, occ_lab = occupancy(alphas, betas, beta_next, blank_lp, lab_lp, log_prob, frame_ok)
        grad_enc, gw_enc, gw_out, d_act_g = joint_backward(enc_out, hidden, soft_probs, occ_blank, occ_lab, lab_ids, w_enc, w_out)
        gw_pred = jnp.einsum('buh,buj->hj', pred_out, d_act_g, preferred_element_type=jnp.float32)
        gw_enc, gw_pred, gw_out = lax.psum((gw_enc, gw_pred, gw_out), 'seq')
        return -log_prob, grad_enc, gw_enc, gw_pred, gw_out

    in_specs = (P('dp', 'seq', None), P('dp', None, None), P(None, None), P(None, None), P(None, None), P('dp', None), P('dp'), P('dp'))
    out_specs = (P('dp'), P('dp', 'seq', None), P('dp', None), P('dp', None), P('dp', None))
    return jax.shard_map(local_fn, mesh=mesh, in_specs=in_specs, out_specs=out_specs, check_vma=False)
```

profile of v0, /device:TPU:80, one launch (start us, length us, event | category | flops | bytes accessed | tf_op | source)
XLA Modules:
  0.0 424.4 jit_solution(9905400477488125448)
XLA Ops:
  8.9 7.8 %convert_convert_fusion = f32[64,64,512]{2,1,0:T(8,128)} fusion(bf16[64,64,512]{2,1,0:T(8,128)(2,1)} %param.21, bf16[512,512]{1,0:T(8,128)(2,1)S(1)} %copy-done), kind=kOutput, calls=%fused_computation.40 | convolution fusion | flops 2151677952 | bytes 13107200 | tf_op jit(solution)/shard_map/buh,hj->buj/dot_general | solution.py:85
  16.6 9.4 %tanh_convert_fusion = bf16[64,2,64,512]{3,2,1,0:T(8,128)(2,1)} fusion(f32[64,64,512]{2,1,0:T(8,128)} %convert_convert_fusion, f32[64,2,512]{2,1,0:T(2,128)S(1)} %copy.46), kind=kLoop, calls=%fused_computation.31 | loop fusion | flops 8388608 | bytes 17039360 | tf_op jit(solution)/shard_map/convert_element_type | solution.py:24
  26.0 7.5 %fusion.45 = (f32[64,2,64]{2,1,0:T(2,128)S(1)}, f32[64,2,64,500]{3,2,1,0:T(8,128)S(1)}) fusion(bf16[64,2,64,512]{3,2,1,0:T(8,128)(2,1)} %tanh_convert_fusion, bf16[512,500]{0,1:T(8,128)(2,1)S(1)} %copy-done.6), kind=kOutput, calls=%fused_computation.86 | convolution fusion | flops 4198391808 | bytes 25317376 | tf_op jit(solution)/shard_map/btuj,jv->btuv/dot_general | solution.py:25
  36.6 4.1 exponential_reduce_fusion
  43.4 17.6 %fusion.12 = f32[64,64,1,2]{3,2,1,0:T(1,128)S(1)} fusion(bf16[64,2,64,512]{3,2,1,0:T(8,128)(2,1)} %tanh_convert_fusion, bf16[64,64,512,1]{2,1,0,3:T(8,128)(2,1)S(1)} %convert_bitcast_fusion), kind=kOutput, calls=%fused_computation.35 | convolution fusion | flops 8388608 | bytes 12615680 | tf_op jit(solution)/shard_map/btuj,buj->btu/dot_general | solution.py:29
  67.9 58.2 %while.108 = (s32[]{:T(128)}, f32[64,64]{1,0:T(8,128)S(1)}, pred[]{:T(512)}, f32[64,2,64]{2,0,1:T(8,128)S(1)}, f32[64,2,64]{2,0,1:T(8,128)S(1)}, /*index=5*/f32[...) while((s32[]{:T(128)}, f32[64,64]{1,0:T(8,128)S(1)}, ...), condition=%wide.region_18.19_spmd.clone, body=%wide.region_13.18_spmd.clone.sunk | while | flops 2330756 | bytes 310835 | solution.py:98
  85.5 4.4 %collective-permute-start = (f32[64,64]{1,0:T(8,128)S(1)}, f32[64,64]{1,0:T(8,128)S(1)}, u32[]{:S(2)}, u32[]{:S(2)}) collective-permute-start(f32[64,64]{1,0:T(8,128)S(1)} %get-tuple-element.1117), channel_id=1, source_target_pairs={{0,1},{1,2},{2,3},{3,4},{4,5},{5,6},{6,7},{8,9},{9,10},{10,11},{11... | collective-permute-start | bytes 49160 | tf_op jit(solution)/shard_map/while/body/eval_jaxpr/ppermute | solution.py:95
  94.4 4.4 %collective-permute-start = (f32[64,64]{1,0:T(8,128)S(1)}, f32[64,64]{1,0:T(8,128)S(1)}, u32[]{:S(2)}, u32[]{:S(2)}) collective-permute-start(f32[64,64]{1,0:T(8,128)S(1)} %get-tuple-element.1117), channel_id=1, source_target_pairs={{0,1},{1,2},{2,3},{3,4},{4,5},{5,6},{6,7},{8,9},{9,10},{10,11},{11... | collective-permute-start | bytes 49160 | tf_op jit(solution)/shard_map/while/body/eval_jaxpr/ppermute | solution.py:95
  103.2 4.4 %collective-permute-start = (f32[64,64]{1,0:T(8,128)S(1)}, f32[64,64]{1,0:T(8,128)S(1)}, u32[]{:S(2)}, u32[]{:S(2)}) collective-permute-start(f32[64,64]{1,0:T(8,128)S(1)} %get-tuple-element.1117), channel_id=1, source_target_pairs={{0,1},{1,2},{2,3},{3,4},{4,5},{5,6},{6,7},{8,9},{9,10},{10,11},{11... | collective-permute-start | bytes 49160 | tf_op jit(solution)/shard_map/while/body/eval_jaxpr/ppermute | solution.py:95
  112.1 4.4 %collective-permute-start = (f32[64,64]{1,0:T(8,128)S(1)}, f32[64,64]{1,0:T(8,128)S(1)}, u32[]{:S(2)}, u32[]{:S(2)}) collective-permute-start(f32[64,64]{1,0:T(8,128)S(1)} %get-tuple-element.1117), channel_id=1, source_target_pairs={{0,1},{1,2},{2,3},{3,4},{4,5},{5,6},{6,7},{8,9},{9,10},{10,11},{11... | collective-permute-start | bytes 49160 | tf_op jit(solution)/shard_map/while/body/eval_jaxpr/ppermute | solution.py:95
  120.9 4.4 %collective-permute-start = (f32[64,64]{1,0:T(8,128)S(1)}, f32[64,64]{1,0:T(8,128)S(1)}, u32[]{:S(2)}, u32[]{:S(2)}) collective-permute-start(f32[64,64]{1,0:T(8,128)S(1)} %get-tuple-element.1117), channel_id=1, source_target_pairs={{0,1},{1,2},{2,3},{3,4},{4,5},{5,6},{6,7},{8,9},{9,10},{10,11},{11... | collective-permute-start | bytes 49160 | tf_op jit(solution)/shard_map/while/body/eval_jaxpr/ppermute | solution.py:95
  126.2 4.0 while.103
  130.3 137.7 %while.105 = (s32[]{:T(128)}, f32[64,64]{1,0:T(8,128)S(1)}, pred[]{:T(512)}, f32[64,2,64]{2,0,1:T(8,128)S(1)}, f32[64,2,64]{2,0,1:T(8,128)S(1)}, /*index=5*/s32[...) while((s32[]{:T(128)}, f32[64,64]{1,0:T(8,128)S(1)}, ...), condition=%wide.region_7.8_spmd.clone, body=%wide.region_2.7_spmd.clone.sunk | while | flops 2351303 | bytes 344355 | solution.py:106
  130.6 14.1 %while.109 = (s32[]{:T(128)}, f32[64,64]{1,0:T(8,128)S(1)}, s32[2]{0:T(128)S(1)}, s32[64]{0:T(128)S(1)}, f32[2,64,64]{2,1,0:T(8,128)S(1)}, /*index=5*/f32[2,64,6...) while((s32[]{:T(128)}, f32[64,64]{1,0:T(8,128)S(1)}, s32[2]{0:T(128)S(1)}, ...), condition=%wide.region_6.6_spmd, body=%wide.region_3.5_spmd.sunk | while | flops 2330819 | bytes 228881 | solution.py:50
  131.0 5.4 %reduce_window.45 = f32[64,64]{1,0:T(8,128)S(1)} reduce-window(f32[64,64]{1,0:T(8,128)S(1)} %fusion.57, f32[]{:T(128)} %constant.190.clone.1..sunk.1..sunk), window={size=1x64 pad=0_0x0_63}, to_apply=%region_5.4 | reduce-window | flops 2064384 | bytes 32772 | tf_op jit(solution)/shard_map/while/body/eval_jaxpr/while/body/eval_jaxpr/reduce_window | solution.py:47
  138.0 5.4 %reduce_window.45 = f32[64,64]{1,0:T(8,128)S(1)} reduce-window(f32[64,64]{1,0:T(8,128)S(1)} %fusion.57, f32[]{:T(128)} %constant.190.clone.1..sunk.1..sunk), window={size=1x64 pad=0_0x0_63}, to_apply=%region_5.4 | reduce-window | flops 2064384 | bytes 32772 | tf_op jit(solution)/shard_map/while/body/eval_jaxpr/while/body/eval_jaxpr/reduce_window | solution.py:47
  150.1 14.1 %while.109 = (s32[]{:T(128)}, f32[64,64]{1,0:T(8,128)S(1)}, s32[2]{0:T(128)S(1)}, s32[64]{0:T(128)S(1)}, f32[2,64,64]{2,1,0:T(8,128)S(1)}, /*index=5*/f32[2,64,6...) while((s32[]{:T(128)}, f32[64,64]{1,0:T(8,128)S(1)}, s32[2]{0:T(128)S(1)}, ...), condition=%wide.region_6.6_spmd, body=%wide.region_3.5_spmd.sunk | while | flops 2330819 | bytes 228881 | solution.py:50
  150.4 5.4 %reduce_window.45 = f32[64,64]{1,0:T(8,128)S(1)} reduce-window(f32[64,64]{1,0:T(8,128)S(1)} %fusion.57, f32[]{:T(128)} %constant.190.clone.1..sunk.1..sunk), window={size=1x64 pad=0_0x0_63}, to_apply=%region_5.4 | reduce-window | flops 2064384 | bytes 32772 | tf_op jit(solution)/shard_map/while/body/eval_jaxpr/while/body/eval_jaxpr/reduce_window | solution.py:47
  157.5 5.4 %reduce_window.45 = f32[64,64]{1,0:T(8,128)S(1)} reduce-window(f32[64,64]{1,0:T(8,128)S(1)} %fusion.57, f32[]{:T(128)} %constant.190.clone.1..sunk.1..sunk), window={size=1x64 pad=0_0x0_63}, to_apply=%region_5.4 | reduce-window | flops 2064384 | bytes 32772 | tf_op jit(solution)/shard_map/while/body/eval_jaxpr/while/body/eval_jaxpr/reduce_window | solution.py:47
  165.5 4.5 %collective-permute-done.1 = f32[64,64]{1,0:T(8,128)S(1)} collective-permute-done((f32[64,64]{1,0:T(8,128)S(1)}, f32[64,64]{1,0:T(8,128)S(1)}, u32[]{:S(2)}, u32[]{:S(2)}) %collective-permute-start.1) | collective-permute-done | bytes 16416 | tf_op jit(solution)/shard_map/while/body/eval_jaxpr/ppermute | solution.py:103
  170.2 14.1 %while.109 = (s32[]{:T(128)}, f32[64,64]{1,0:T(8,128)S(1)}, s32[2]{0:T(128)S(1)}, s32[64]{0:T(128)S(1)}, f32[2,64,64]{2,1,0:T(8,128)S(1)}, /*index=5*/f32[2,64,6...) while((s32[]{:T(128)}, f32[64,64]{1,0:T(8,128)S(1)}, s32[2]{0:T(128)S(1)}, ...), condition=%wide.region_6.6_spmd, body=%wide.region_3.5_spmd.sunk | while | flops 2330819 | bytes 228881 | solution.py:50
  170.5 5.4 %reduce_window.45 = f32[64,64]{1,0:T(8,128)S(1)} reduce-window(f32[64,64]{1,0:T(8,128)S(1)} %fusion.57, f32[]{:T(128)} %constant.190.clone.1..sunk.1..sunk), window={size=1x64 pad=0_0x0_63}, to_apply=%region_5.4 | reduce-window | flops 2064384 | bytes 32772 | tf_op jit(solution)/shard_map/while/body/eval_jaxpr/while/body/eval_jaxpr/reduce_window | solution.py:47
  177.6 5.4 %reduce_window.45 = f32[64,64]{1,0:T(8,128)S(1)} reduce-window(f32[64,64]{1,0:T(8,128)S(1)} %fusion.57, f32[]{:T(128)} %constant.190.clone.1..sunk.1..sunk), window={size=1x64 pad=0_0x0_63}, to_apply=%region_5.4 | reduce-window | flops 2064384 | bytes 32772 | tf_op jit(solution)/shard_map/while/body/eval_jaxpr/while/body/eval_jaxpr/reduce_window | solution.py:47
  185.7 3.9 collective-permute-done.1
  189.8 14.1 %while.109 = (s32[]{:T(128)}, f32[64,64]{1,0:T(8,128)S(1)}, s32[2]{0:T(128)S(1)}, s32[64]{0:T(128)S(1)}, f32[2,64,64]{2,1,0:T(8,128)S(1)}, /*index=5*/f32[2,64,6...) while((s32[]{:T(128)}, f32[64,64]{1,0:T(8,128)S(1)}, s32[2]{0:T(128)S(1)}, ...), condition=%wide.region_6.6_spmd, body=%wide.region_3.5_spmd.sunk | while | flops 2330819 | bytes 228881 | solution.py:50
  190.1 5.4 %reduce_window.45 = f32[64,64]{1,0:T(8,128)S(1)} reduce-window(f32[64,64]{1,0:T(8,128)S(1)} %fusion.57, f32[]{:T(128)} %constant.190.clone.1..sunk.1..sunk), window={size=1x64 pad=0_0x0_63}, to_apply=%region_5.4 | reduce-window | flops 2064384 | bytes 32772 | tf_op jit(solution)/shard_map/while/body/eval_jaxpr/while/body/eval_jaxpr/reduce_window | solution.py:47
  197.2 5.4 %reduce_window.45 = f32[64,64]{1,0:T(8,128)S(1)} reduce-window(f32[64,64]{1,0:T(8,128)S(1)} %fusion.57, f32[]{:T(128)} %constant.190.clone.1..sunk.1..sunk), window={size=1x64 pad=0_0x0_63}, to_apply=%region_5.4 | reduce-window | flops 2064384 | bytes 32772 | tf_op jit(solution)/shard_map/while/body/eval_jaxpr/while/body/eval_jaxpr/reduce_window | solution.py:47
  205.2 3.9 collective-permute-done.1
  209.4 14.1 %while.109 = (s32[]{:T(128)}, f32[64,64]{1,0:T(8,128)S(1)}, s32[2]{0:T(128)S(1)}, s32[64]{0:T(128)S(1)}, f32[2,64,64]{2,1,0:T(8,128)S(1)}, /*index=5*/f32[2,64,6...) while((s32[]{:T(128)}, f32[64,64]{1,0:T(8,128)S(1)}, s32[2]{0:T(128)S(1)}, ...), condition=%wide.region_6.6_spmd, body=%wide.region_3.5_spmd.sunk | while | flops 2330819 | bytes 228881 | solution.py:50
  209.7 5.4 %reduce_window.45 = f32[64,64]{1,0:T(8,128)S(1)} reduce-window(f32[64,64]{1,0:T(8,128)S(1)} %fusion.57, f32[]{:T(128)} %constant.190.clone.1..sunk.1..sunk), window={size=1x64 pad=0_0x0_63}, to_apply=%region_5.4 | reduce-window | flops 2064384 | bytes 32772 | tf_op jit(solution)/shard_map/while/body/eval_jaxpr/while/body/eval_jaxpr/reduce_window | solution.py:47
  216.8 5.4 %reduce_window.45 = f32[64,64]{1,0:T(8,128)S(1)} reduce-window(f32[64,64]{1,0:T(8,128)S(1)} %fusion.57, f32[]{:T(128)} %constant.190.clone.1..sunk.1..sunk), window={size=1x64 pad=0_0x0_63}, to_apply=%region_5.4 | reduce-window | flops 2064384 | bytes 32772 | tf_op jit(solution)/shard_map/while/body/eval_jaxpr/while/body/eval_jaxpr/reduce_window | solution.py:47
  224.8 3.9 collective-permute-done.1
  228.9 14.1 %while.109 = (s32[]{:T(128)}, f32[64,64]{1,0:T(8,128)S(1)}, s32[2]{0:T(128)S(1)}, s32[64]{0:T(128)S(1)}, f32[2,64,64]{2,1,0:T(8,128)S(1)}, /*index=5*/f32[2,64,6...) while((s32[]{:T(128)}, f32[64,64]{1,0:T(8,128)S(1)}, s32[2]{0:T(128)S(1)}, ...), condition=%wide.region_6.6_spmd, body=%wide.region_3.5_spmd.sunk | while | flops 2330819 | bytes 228881 | solution.py:50
  229.3 5.4 %reduce_window.45 = f32[64,64]{1,0:T(8,128)S(1)} reduce-window(f32[64,64]{1,0:T(8,128)S(1)} %fusion.57, f32[]{:T(128)} %constant.190.clone.1..sunk.1..sunk), window={size=1x64 pad=0_0x0_63}, to_apply=%region_5.4 | reduce-window | flops 2064384 | bytes 32772 | tf_op jit(solution)/shard_map/while/body/eval_jaxpr/while/body/eval_jaxpr/reduce_window | solution.py:47
  236.3 5.4 %reduce_window.45 = f32[64,64]{1,0:T(8,128)S(1)} reduce-window(f32[64,64]{1,0:T(8,128)S(1)} %fusion.57, f32[]{:T(128)} %constant.190.clone.1..sunk.1..sunk), window={size=1x64 pad=0_0x0_63}, to_apply=%region_5.4 | reduce-window | flops 2064384 | bytes 32772 | tf_op jit(solution)/shard_map/while/body/eval_jaxpr/while/body/eval_jaxpr/reduce_window | solution.py:47
  244.4 3.9 collective-permute-done.1
  248.5 14.1 %while.109 = (s32[]{:T(128)}, f32[64,64]{1,0:T(8,128)S(1)}, s32[2]{0:T(128)S(1)}, s32[64]{0:T(128)S(1)}, f32[2,64,64]{2,1,0:T(8,128)S(1)}, /*index=5*/f32[2,64,6...) while((s32[]{:T(128)}, f32[64,64]{1,0:T(8,128)S(1)}, s32[2]{0:T(128)S(1)}, ...), condition=%wide.region_6.6_spmd, body=%wide.region_3.5_spmd.sunk | while | flops 2330819 | bytes 228881 | solution.py:50
  248.8 5.4 %reduce_window.45 = f32[64,64]{1,0:T(8,128)S(1)} reduce-window(f32[64,64]{1,0:T(8,128)S(1)} %fusion.57, f32[]{:T(128)} %constant.190.clone.1..sunk.1..sunk), window={size=1x64 pad=0_0x0_63}, to_apply=%region_5.4 | reduce-window | flops 2064384 | bytes 32772 | tf_op jit(solution)/shard_map/while/body/eval_jaxpr/while/body/eval_jaxpr/reduce_window | solution.py:47
  255.9 5.4 %reduce_window.45 = f32[64,64]{1,0:T(8,128)S(1)} reduce-window(f32[64,64]{1,0:T(8,128)S(1)} %fusion.57, f32[]{:T(128)} %constant.190.clone.1..sunk.1..sunk), window={size=1x64 pad=0_0x0_63}, to_apply=%region_5.4 | reduce-window | flops 2064384 | bytes 32772 | tf_op jit(solution)/shard_map/while/body/eval_jaxpr/while/body/eval_jaxpr/reduce_window | solution.py:47
  268.0 15.1 %while.106 = (s32[]{:T(128)}, f32[64,64]{1,0:T(8,128)S(1)}, f32[2,64,64]{2,0,1:T(2,128)S(1)}, f32[2,64,64]{2,0,1:T(2,128)S(1)}, s32[2]{0:T(128)S(1)}, /*index=5*...) while((s32[]{:T(128)}, f32[64,64]{1,0:T(8,128)S(1)}, ...), condition=%wide.region_11.12_spmd.clone, body=%wide.region_8.11_spmd.clone.sunk | while | flops 2339011 | bytes 278321 | solution.py:50
  268.4 5.4 %reduce_window.43 = f32[64,64]{1,0:T(8,128)S(1)} reduce-window(f32[64,64]{1,0:T(8,128)S(1)} %fusion.56, f32[]{:T(128)} %constant.190.clone.1..sunk.2), window={size=1x64 pad=0_0x0_63}, to_apply=%region_10.10 | reduce-window | flops 2064384 | bytes 32772 | tf_op jit(solution)/shard_map/while/body/eval_jaxpr/reduce_window | solution.py:47
  275.8 5.4 %reduce_window.43 = f32[64,64]{1,0:T(8,128)S(1)} reduce-window(f32[64,64]{1,0:T(8,128)S(1)} %fusion.56, f32[]{:T(128)} %constant.190.clone.1..sunk.2), window={size=1x64 pad=0_0x0_63}, to_apply=%region_10.10 | reduce-window | flops 2064384 | bytes 32772 | tf_op jit(solution)/shard_map/while/body/eval_jaxpr/reduce_window | solution.py:47
  283.4 15.1 %psum.28 = f32[64]{0:T(128)S(1)} all-reduce(f32[64]{0:T(128)S(1)} %select_reduce_fusion), channel_id=1, replica_groups=mesh['dp'=4,'seq'=8] {'seq'}, use_global_device_ids=true, to_apply=%region_12.13 | all-reduce | flops 64 | bytes 512 | tf_op jit(solution)/shard_map/psum | solution.py:108
  298.8 14.7 %convolution_bitcast_fusion.2 = f32[512,500]{0,1:T(8,128)} fusion(bf16[64,2,64,512]{3,2,1,0:T(8,128)(2,1)} %tanh_convert_fusion, f32[64,2,64,500]{3,2,1,0:T(8,128)} %copy-done.2, f32[64,2,64]{2,1,0:T(2,128)S(1)} %get-tuple-element.851, f32[64,2,64]{2,1,0:T(2,128)S(1)} %get-tuple-element.850, f32[64,2,64]{2,1,0:T(2,128)S(1)} %get-tuple-element.849, ...), kind=kOutput, calls=%fused_computation.43 | convolution fusion | flops 4222976000 | bytes 27976180 | tf_op jit(solution)/shard_map/btuj,btuv->jv/dot_general | solution.py:71
  313.4 16.3 %fusion.46 = (bf16[64,2,512]{2,1,0:T(2,128)(2,1)S(1)}, bf16[64,2,64,512]{3,2,1,0:T(8,128)(2,1)}) fusion(bf16[64,2,64,512]{3,2,1,0:T(8,128)(2,1)} %tanh_convert_fusion, bf16[512,500]{0,1:T(8,128)(2,1)S(1)} %copy-done.6, f32[64,2,64,500]{3,2,1,0:T(8,128)} %copy-done.2, f32[64,2,64]{2,1,0:T(2,128)S(1)} %get-tuple-element.851, ...), kind=kOutput, calls=%fused_computation.87 | convolution fusion | flops 4248076288 | bytes 35983860 | tf_op jit(solution)/shard_map/btuv,jv->btuj/dot_general | solution.py:65
  329.7 9.2 %convert_reduce_fusion = bf16[64,64,512]{2,1,0:T(8,128)(2,1)} fusion(bf16[64,2,64,512]{3,2,1,0:T(8,128)(2,1)} %get-tuple-element.857), kind=kLoop, calls=%fused_computation.27 | loop fusion | flops 6291456 | bytes 12582912 | tf_op jit(solution)/shard_map/reduce_sum | solution.py:68
  338.9 5.6 %convolution_bitcast_fusion = f32[512,512]{0,1:T(8,128)} fusion(bf16[64,64,512]{2,1,0:T(8,128)(2,1)} %convert_reduce_fusion, bf16[64,64,512]{2,1,0:T(8,128)(2,1)S(1)} %copy-done.3), kind=kOutput, calls=%fused_computation.41 | convolution fusion | flops 2147483648 | bytes 9437184 | tf_op jit(solution)/shard_map/buh,buj->hj/dot_general | solution.py:112
  347.5 62.3 %all-reduce.9.cloned.1.call-done = (f32[512,512]{0,1:T(8,128)}, f32[512,512]{0,1:T(8,128)}, f32[512,500]{0,1:T(8,128)}) async-done(((f32[512,512]{0,1:T(8,128)}, f32[512,512]{0,1:T(8,128)}, f32[512,500]{0,1:T(8,128)}), (f32[512,512]{0,1:T(8,128)}, f32[512,512]{0,1:T(8,128)}, f32[512,500]{0,1:T(8,128)})) %all-reduce.9.cloned.1.call-update) | async-done | bytes 3121168 | tf_op jit(solution)/shard_map/psum | solution.py:113
  (292 shorter events, 134.7 us)
Async XLA Ops:
  7.2 1.7 copy-start
  7.2 402.6 %all-reduce.9.cloned.1.call-start = ((), (), s32[]{:S(2)}) async-start(), calls=%async_computation | async-start | bytes 6258688 | tf_op jit(solution)/shard_map/psum | solution.py:113
  16.6 9.4 %copy-start.6 = (bf16[512,500]{0,1:T(8,128)(2,1)S(1)}, bf16[512,500]{0,1:T(8,128)(2,1)}, u32[]{:S(2)}) copy-start(bf16[512,500]{0,1:T(8,128)(2,1)} %param.24) | copy-start | bytes 1536004
  33.5 7.2 %copy-start.2 = (f32[64,2,64,500]{3,2,1,0:T(8,128)}, f32[64,2,64,500]{3,2,1,0:T(8,128)S(1)}, u32[]{:S(2)}) copy-start(f32[64,2,64,500]{3,2,1,0:T(8,128)S(1)} %get-tuple-element.855) | copy-start | bytes 49152004
  36.6 4.1 copy-start.8
  67.9 62.2 %copy-start.7 = (s32[64]{0:T(128)S(1)}, s32[64]{0:T(128)}, u32[]{:S(2)}) copy-start(s32[64]{0:T(128)} %param.27) | copy-start | bytes 772
  67.9 62.3 %copy-start.9 = (s32[64]{0:T(128)S(1)}, s32[64]{0:T(128)}, u32[]{:S(2)}) copy-start(s32[64]{0:T(128)} %param.26) | copy-start | bytes 772
  71.5 2.2 collective-permute-start
  77.3 4.7 %collective-permute-start = (f32[64,64]{1,0:T(8,128)S(1)}, f32[64,64]{1,0:T(8,128)S(1)}, u32[]{:S(2)}, u32[]{:S(2)}) collective-permute-start(f32[64,64]{1,0:T(8,128)S(1)} %get-tuple-element.1117), channel_id=1, source_target_pairs={{0,1},{1,2},{2,3},{3,4},{4,5},{5,6},{6,7},{8,9},{9,10},{10,11},{11... | collective-permute-start | bytes 49160 | tf_op jit(solution)/shard_map/while/body/eval_jaxpr/ppermute | solution.py:95
  85.5 5.3 %collective-permute-start = (f32[64,64]{1,0:T(8,128)S(1)}, f32[64,64]{1,0:T(8,128)S(1)}, u32[]{:S(2)}, u32[]{:S(2)}) collective-permute-start(f32[64,64]{1,0:T(8,128)S(1)} %get-tuple-element.1117), channel_id=1, source_target_pairs={{0,1},{1,2},{2,3},{3,4},{4,5},{5,6},{6,7},{8,9},{9,10},{10,11},{11... | collective-permute-start | bytes 49160 | tf_op jit(solution)/shard_map/while/body/eval_jaxpr/ppermute | solution.py:95
  94.4 5.3 %collective-permute-start = (f32[64,64]{1,0:T(8,128)S(1)}, f32[64,64]{1,0:T(8,128)S(1)}, u32[]{:S(2)}, u32[]{:S(2)}) collective-permute-start(f32[64,64]{1,0:T(8,128)S(1)} %get-tuple-element.1117), channel_id=1, source_target_pairs={{0,1},{1,2},{2,3},{3,4},{4,5},{5,6},{6,7},{8,9},{9,10},{10,11},{11... | collective-permute-start | bytes 49160 | tf_op jit(solution)/shard_map/while/body/eval_jaxpr/ppermute | solution.py:95
  103.2 5.3 %collective-permute-start = (f32[64,64]{1,0:T(8,128)S(1)}, f32[64,64]{1,0:T(8,128)S(1)}, u32[]{:S(2)}, u32[]{:S(2)}) collective-permute-start(f32[64,64]{1,0:T(8,128)S(1)} %get-tuple-element.1117), channel_id=1, source_target_pairs={{0,1},{1,2},{2,3},{3,4},{4,5},{5,6},{6,7},{8,9},{9,10},{10,11},{11... | collective-permute-start | bytes 49160 | tf_op jit(solution)/shard_map/while/body/eval_jaxpr/ppermute | solution.py:95
  112.1 5.3 %collective-permute-start = (f32[64,64]{1,0:T(8,128)S(1)}, f32[64,64]{1,0:T(8,128)S(1)}, u32[]{:S(2)}, u32[]{:S(2)}) collective-permute-start(f32[64,64]{1,0:T(8,128)S(1)} %get-tuple-element.1117), channel_id=1, source_target_pairs={{0,1},{1,2},{2,3},{3,4},{4,5},{5,6},{6,7},{8,9},{9,10},{10,11},{11... | collective-permute-start | bytes 49160 | tf_op jit(solution)/shard_map/while/body/eval_jaxpr/ppermute | solution.py:95
  120.9 5.3 %collective-permute-start = (f32[64,64]{1,0:T(8,128)S(1)}, f32[64,64]{1,0:T(8,128)S(1)}, u32[]{:S(2)}, u32[]{:S(2)}) collective-permute-start(f32[64,64]{1,0:T(8,128)S(1)} %get-tuple-element.1117), channel_id=1, source_target_pairs={{0,1},{1,2},{2,3},{3,4},{4,5},{5,6},{6,7},{8,9},{9,10},{10,11},{11... | collective-permute-start | bytes 49160 | tf_op jit(solution)/shard_map/while/body/eval_jaxpr/ppermute | solution.py:95
  144.8 5.1 %collective-permute-start.1 = (f32[64,64]{1,0:T(8,128)S(1)}, f32[64,64]{1,0:T(8,128)S(1)}, u32[]{:S(2)}, u32[]{:S(2)}) collective-permute-start(f32[64,64]{1,0:T(8,128)S(1)} %get-tuple-element.1100), channel_id=1, source_target_pairs={{1,0},{2,1},{3,2},{4,3},{5,4},{6,5},{7,6},{9,8},{10,9},{11,10},{12... | collective-permute-start | bytes 49160 | tf_op jit(solution)/shard_map/while/body/eval_jaxpr/ppermute | solution.py:103
  164.2 5.8 %collective-permute-start.1 = (f32[64,64]{1,0:T(8,128)S(1)}, f32[64,64]{1,0:T(8,128)S(1)}, u32[]{:S(2)}, u32[]{:S(2)}) collective-permute-start(f32[64,64]{1,0:T(8,128)S(1)} %get-tuple-element.1100), channel_id=1, source_target_pairs={{1,0},{2,1},{3,2},{4,3},{5,4},{6,5},{7,6},{9,8},{10,9},{11,10},{12... | collective-permute-start | bytes 49160 | tf_op jit(solution)/shard_map/while/body/eval_jaxpr/ppermute | solution.py:103
  184.4 5.3 %collective-permute-start.1 = (f32[64,64]{1,0:T(8,128)S(1)}, f32[64,64]{1,0:T(8,128)S(1)}, u32[]{:S(2)}, u32[]{:S(2)}) collective-permute-start(f32[64,64]{1,0:T(8,128)S(1)} %get-tuple-element.1100), channel_id=1, source_target_pairs={{1,0},{2,1},{3,2},{4,3},{5,4},{6,5},{7,6},{9,8},{10,9},{11,10},{12... | collective-permute-start | bytes 49160 | tf_op jit(solution)/shard_map/while/body/eval_jaxpr/ppermute | solution.py:103
  203.9 5.3 %collective-permute-start.1 = (f32[64,64]{1,0:T(8,128)S(1)}, f32[64,64]{1,0:T(8,128)S(1)}, u32[]{:S(2)}, u32[]{:S(2)}) collective-permute-start(f32[64,64]{1,0:T(8,128)S(1)} %get-tuple-element.1100), channel_id=1, source_target_pairs={{1,0},{2,1},{3,2},{4,3},{5,4},{6,5},{7,6},{9,8},{10,9},{11,10},{12... | collective-permute-start | bytes 49160 | tf_op jit(solution)/shard_map/while/body/eval_jaxpr/ppermute | solution.py:103
  223.5 5.3 %collective-permute-start.1 = (f32[64,64]{1,0:T(8,128)S(1)}, f32[64,64]{1,0:T(8,128)S(1)}, u32[]{:S(2)}, u32[]{:S(2)}) collective-permute-start(f32[64,64]{1,0:T(8,128)S(1)} %get-tuple-element.1100), channel_id=1, source_target_pairs={{1,0},{2,1},{3,2},{4,3},{5,4},{6,5},{7,6},{9,8},{10,9},{11,10},{12... | collective-permute-start | bytes 49160 | tf_op jit(solution)/shard_map/while/body/eval_jaxpr/ppermute | solution.py:103
  243.1 5.3 %collective-permute-start.1 = (f32[64,64]{1,0:T(8,128)S(1)}, f32[64,64]{1,0:T(8,128)S(1)}, u32[]{:S(2)}, u32[]{:S(2)}) collective-permute-start(f32[64,64]{1,0:T(8,128)S(1)} %get-tuple-element.1100), channel_id=1, source_target_pairs={{1,0},{2,1},{3,2},{4,3},{5,4},{6,5},{7,6},{9,8},{10,9},{11,10},{12... | collective-permute-start | bytes 49160 | tf_op jit(solution)/shard_map/while/body/eval_jaxpr/ppermute | solution.py:103
  262.7 5.3 %collective-permute-start.1 = (f32[64,64]{1,0:T(8,128)S(1)}, f32[64,64]{1,0:T(8,128)S(1)}, u32[]{:S(2)}, u32[]{:S(2)}) collective-permute-start(f32[64,64]{1,0:T(8,128)S(1)} %get-tuple-element.1100), channel_id=1, source_target_pairs={{1,0},{2,1},{3,2},{4,3},{5,4},{6,5},{7,6},{9,8},{10,9},{11,10},{12... | collective-permute-start | bytes 49160 | tf_op jit(solution)/shard_map/while/body/eval_jaxpr/ppermute | solution.py:103
  329.7 9.2 %copy-start.3 = (bf16[64,64,512]{2,1,0:T(8,128)(2,1)S(1)}, bf16[64,64,512]{2,1,0:T(8,128)(2,1)}, u32[]{:S(2)}) copy-start(bf16[64,64,512]{2,1,0:T(8,128)(2,1)} %param.21) | copy-start | bytes 12582916
  338.9 5.6 %copy-start.5 = (bf16[64,2,512]{2,1,0:T(2,128)(2,1)S(1)}, bf16[64,2,512]{2,1,0:T(2,128)(2,1)}, u32[]{:S(2)}) copy-start(bf16[64,2,512]{2,1,0:T(2,128)(2,1)} %param.20) | copy-start | bytes 393220
  338.9 7.5 %copy-start.4 = (bf16[512,512]{1,0:T(8,128)(2,1)S(1)}, bf16[512,512]{1,0:T(8,128)(2,1)}, u32[]{:S(2)}) copy-start(bf16[512,512]{1,0:T(8,128)(2,1)} %param.22) | copy-start | bytes 1572868
  338.9 78.2 %copy-start.1 = (bf16[512,512]{1,0:T(8,128)(2,1)S(1)}, bf16[512,512]{1,0:T(8,128)(2,1)}, u32[]{:S(2)}) copy-start(bf16[512,512]{1,0:T(8,128)(2,1)} %param.23) | copy-start | bytes 1572868
Sparse Core Ops, SparseCore 0:
  346.0 63.7 all-reduce.8
where the time goes:
time: 429 us; the launch traced here: 424 us
  other arithmetic  158 us (37%)
  waiting for transfers between devices  96.3 us (22%)
  matrix products  75 us (17%)
  starting transfers between devices  36.4 us (8%)
  local copies, waits for them, and re-layouts  27.4 us (6%)
  blocking collectives  15.1 us (4%)
  between operations  14.8 us (3%)
    another operation x16, other arithmetic, frame_step(): lax.cumlogsumexp(next_row + frame_blank + lab_sum, axis=1, reverse=True)  86.5 us
    psum x1, waiting for transfers between devices, local_fn(): gw_enc, gw_pred, gw_out = lax.psum((gw_enc, gw_pred, gw_out), 'seq')  62.3 us
    ppermute x7, waiting for transfers between devices, beta_hop(): received = lax.ppermute(first_row, 'seq', bwd_pairs)  28.1 us
    ppermute x7, starting transfers between devices, alpha_hop(): received = lax.ppermute(x_out, 'seq', fwd_pairs)  27.2 us
    another operation x16, other arithmetic, frame_step(): alpha_t = lab_sum + lax.cumlogsumexp(x_prev - lab_sum, axis=1)  22 us
    dot_general x1, matrix products, joint_lattice(): jnp.einsum('btuj,buj->btu', hidden, lab_w, preferred_element_type=jnp.flo...  17.6 us
    dot_general x1, matrix products, joint_backward(): jnp.einsum('btuv,jv->btuj', d_logits, w_out, preferred_element_type=jnp.f...  16.3 us
    psum x1, blocking collectives, local_fn(): log_prob = lax.psum(jnp.where(seq_idx == 0, first_row[:, 0], 0.0), 'seq')  15.1 us
  transfers between devices with their start and end apart: 15, of which 15 were waited for; matrix products, arithmetic and copies ran while one was open for 0% of the time, Pallas kernels for 0%

commit v1 on v0

v1 whole, which is shorter than its diff:
```python
import functools

import jax
import jax.numpy as jnp
from jax import lax
from jax.experimental import pallas as pl
from jax.experimental.pallas import tpu as pltpu
from jax.sharding import PartitionSpec as P

NEG_FILL = -1.0e30
CHUNK = 16
LANES = 128
TILE_CHUNKS = 16
TILE = CHUNK * TILE_CHUNKS
F32 = jnp.float32
BF16 = jnp.bfloat16


def logadd(x, y):
    return jnp.maximum(x, y) + jnp.log(1.0 + jnp.exp(-jnp.abs(x - y)))


def dot_nn(x, y):
    return jnp.dot(x, y, preferred_element_type=F32)


def dot_tn(x, y):
    return lax.dot_general(x, y, (((0,), (0,)), ((), ())), preferred_element_type=F32)


def dot_nt(x, y):
    return lax.dot_general(x, y, (((1,), (1,)), ((), ())), preferred_element_type=F32)


def local_kernel(n_utt, n_frames, n_pos, vocab,
                 seq_ref, tlen_ref, ulen_ref,
                 enc_hbm, pred_hbm, wenc_hbm, wpred_hbm, wout_hbm, labels_ref,
                 loss_ref, genc_ref, gwe_ref, gwp_ref, gwo_ref,
                 f_v, g_v, we_v, wp_v, wo_v, wt_v, act_f, act_g, lab_v, lab_scr,
                 hid, ex, sums, sk_b, sk_l, al, xb_s, xl_s, occ_b, occ_l, dz_v, dh_v,
                 dc, da8, lrow, arow, sbase, gbase, utt_of, sems):
    me = seq_ref[0]
    n_diag = n_frames + n_pos - 1
    skew_rows = (n_frames + n_pos) * n_frames
    n_rows = n_utt * n_pos
    vocab_pad = wo_v.shape[1]
    n_grp = vocab_pad // LANES

    copies = [
        pltpu.make_async_copy(enc_hbm, f_v, sems.at[0]),
        pltpu.make_async_copy(pred_hbm.at[pl.ds(pl.multiple_of(me * n_rows, n_rows), n_rows), :], g_v, sems.at[1]),
        pltpu.make_async_copy(wenc_hbm, we_v, sems.at[2]),
        pltpu.make_async_copy(wpred_hbm, wp_v, sems.at[3]),
        pltpu.make_async_copy(wout_hbm, wo_v, sems.at[4]),
    ]
    for cp in copies:
        cp.start()

    def add_utt(b, pos):
        t_len = tlen_ref[me * n_utt + b]
        n_chunk = (ulen_ref[me * n_utt + b] + CHUNK) // CHUNK

        def add_frame(t, pos):
            def add_chunk(q, pos):
                lrow[pos] = b * n_pos + q * CHUNK
                arow[pos] = b * n_frames + t
                skew = (n_frames + 1) * t + n_frames * CHUNK * q
                sbase[pos] = b * skew_rows + skew
                gbase[pos] = skew
                utt_of[pos] = b
                return pos + 1
            return lax.fori_loop(0, n_chunk, add_chunk, pos)
        return lax.fori_loop(0, t_len, add_frame, pos)

    n_chunks = lax.fori_loop(0, n_utt, add_utt, 0)
    n_tiles = (n_chunks + TILE_CHUNKS - 1) // TILE_CHUNKS

    def add_dummy(pos, carry):
        lrow[pos] = n_rows
        arow[pos] = n_utt * n_frames
        sbase[pos] = n_utt * skew_rows
        gbase[pos] = skew_rows
        utt_of[pos] = 0
        return carry
    lax.fori_loop(n_chunks, n_tiles * TILE_CHUNKS, add_dummy, 0)

    dc[...] = jnp.zeros_like(dc)
    da8[...] = jnp.zeros_like(da8)
    gwo_ref[...] = jnp.zeros_like(gwo_ref)
    occ_b[pl.ds(skew_rows, 256), :] = jnp.zeros((256, LANES), F32)
    occ_l[pl.ds(skew_rows, 256), :] = jnp.zeros((256, LANES), F32)
    act_f[pl.ds(n_utt * n_frames, 8), :] = jnp.zeros((8, act_f.shape[1]), F32)
    act_g[pl.ds(n_rows, CHUNK), :] = jnp.zeros((CHUNK, act_g.shape[1]), BF16)
    lab_v[pl.ds(n_rows, CHUNK), :] = jnp.full((CHUNK, LANES), -1, jnp.int32)

    lab_scr[...] = jnp.full_like(lab_scr, -1.0)
    lab_scr[:, :n_pos - 1] = labels_ref[pl.ds(pl.multiple_of(me * n_utt, n_utt), n_utt), :].astype(F32)
    lab_t = jnp.transpose(lab_scr[...])
    for b in range(n_utt):
        lab_v[pl.ds(b * n_pos, n_pos), :] = jnp.broadcast_to(lab_t[:n_pos, b:b + 1], (n_pos, LANES)).astype(jnp.int32)

    for cp in copies:
        cp.wait()
    act_f[pl.ds(0, n_utt * n_frames), :] = dot_nn(f_v[...], we_v[...]).astype(BF16).astype(F32)
    act_g[pl.ds(0, n_rows), :] = dot_nn(g_v[...], wp_v[...]).astype(BF16)
    wt_v[...] = jnp.transpose(wo_v[...])

    lane = lax.broadcasted_iota(jnp.int32, (CHUNK, LANES), 1)
    last_ok = lane < vocab - (n_grp - 1) * LANES

    def fwd_tile(i, carry):
        r0 = pl.multiple_of(i * TILE, TILE)
        for k in range(TILE_CHUNKS):
            lr = pl.multiple_of(lrow[i * TILE_CHUNKS + k], CHUNK)
            ar = arow[i * TILE_CHUNKS + k]
            pre = act_g[pl.ds(lr, CHUNK), :].astype(F32) + act_f[pl.ds(ar, 1), :]
            hid[pl.ds(r0 + k * CHUNK, CHUNK), :] = jnp.tanh(pre).astype(BF16)
        ex[pl.ds(r0, TILE), :] = dot_nn(hid[pl.ds(r0, TILE), :], wo_v[...])
        for k in range(TILE_CHUNKS):
            rows = pl.ds(r0 + k * CHUNK, CHUNK)
            lr = pl.multiple_of(lrow[i * TILE_CHUNKS + k], CHUNK)
            sb = sbase[i * TILE_CHUNKS + k]
            ids = lab_v[pl.ds(lr, CHUNK), :]
            zs = [ex[rows, j * LANES:(j + 1) * LANES] for j in range(n_grp)]
            zs[-1] = jnp.where(last_ok, zs[-1], NEG_FILL)
            top = functools.reduce(jnp.maximum, zs)
            top = jnp.max(top, axis=1, keepdims=True)
            picked = functools.reduce(jnp.add, [jnp.where(lane + j * LANES == ids, zs[j], 0.0) for j in range(n_grp)])
            picked = jnp.sum(picked, axis=1, keepdims=True)
            es = [jnp.exp(z - top) for z in zs]
            for j in range(n_grp):
                ex[rows, j * LANES:(j + 1) * LANES] = es[j]
            tot = jnp.sum(functools.reduce(jnp.add, es), axis=1, keepdims=True)
            tot_b = jnp.broadcast_to(tot, (CHUNK, LANES))
            sums[rows, :] = tot_b
            log_norm = top + jnp.log(tot_b)
            sk_b[pl.ds(sb, CHUNK, stride=n_frames), :] = zs[0][:, 0:1] - log_norm
            sk_l[pl.ds(sb, CHUNK, stride=n_frames), :] = picked - log_norm
        return carry
    lax.fori_loop(0, n_tiles, fwd_tile, 0)

    lane_s = lax.broadcasted_iota(jnp.int32, (n_frames, LANES), 1)
    sub_s = lax.broadcasted_iota(jnp.int32, (n_frames, LANES), 0)
    t_lens = jnp.zeros((n_frames, LANES), jnp.int32)
    u_lens = jnp.zeros((n_frames, LANES), jnp.int32)
    for b in range(n_utt):
        t_lens = jnp.where(lane_s == b, tlen_ref[me * n_utt + b], t_lens)
        u_lens = jnp.where(lane_s == b, ulen_ref[me * n_utt + b], u_lens)
    live_t = sub_s < t_lens
    last_t = sub_s == t_lens - 1

    def diag(d):
        base = pl.multiple_of(d * n_frames, n_frames)
        bl = sk_b[pl.ds(base, n_frames), :]
        lb = sk_l[pl.ds(base, n_frames), :]
        for b in range(1, n_utt):
            off = pl.multiple_of(base + b * skew_rows, n_frames)
            bl = jnp.where(lane_s == b, sk_b[pl.ds(off, n_frames), :], bl)
            lb = jnp.where(lane_s == b, sk_l[pl.ds(off, n_frames), :], lb)
        u = d - sub_s
        live = live_t & (u >= 0)
        bl = jnp.where(live & (u <= u_lens), bl, NEG_FILL)
        lb = jnp.where(live & (u < u_lens), lb, NEG_FILL)
        return base, bl, lb, last_t & (u == u_lens)

    def lattice_step(i, carry):
        a, be = carry
        base, bl, lb, _ = diag(i)
        al[pl.ds(base, n_frames), :] = a
        moved = jnp.where(sub_s == 0, NEG_FILL, pltpu.roll(a + bl, 1, 0))
        a = logadd(moved, a + lb)
        base, bl, lb, end = diag(n_diag - 1 - i)
        up = jnp.where(sub_s == n_frames - 1, NEG_FILL, pltpu.roll(be, n_frames - 1, 0))
        x_b = jnp.where(end, bl, up + bl)
        x_l = be + lb
        xb_s[pl.ds(base, n_frames), :] = x_b
        xl_s[pl.ds(base, n_frames), :] = x_l
        return a, logadd(x_b, x_l)

    neg = jnp.full((n_frames, LANES), NEG_FILL, F32)
    _, be0 = lax.fori_loop(0, n_diag, lattice_step, (jnp.where(sub_s == 0, 0.0, neg), neg))
    log_prob = be0[0:1, :]
    loss_ref[...] = jnp.broadcast_to(-log_prob, loss_ref.shape)

    n_live = n_diag * n_frames
    for r in range(0, n_live, 64):
        rows = pl.ds(r, min(64, n_live - r))
        a = al[rows, :] - log_prob
        occ_b[rows, :] = jnp.exp(jnp.minimum(a + xb_s[rows, :], 0.0))
        occ_l[rows, :] = jnp.exp(jnp.minimum(a + xl_s[rows, :], 0.0))

    def bwd_tile(i, carry):
        r0 = pl.multiple_of(i * TILE, TILE)
        for k in range(TILE_CHUNKS):
            rows = pl.ds(r0 + k * CHUNK, CHUNK)
            lr = pl.multiple_of(lrow[i * TILE_CHUNKS + k], CHUNK)
            gb0 = gbase[i * TILE_CHUNKS + k]
            mine = lane == utt_of[i * TILE_CHUNKS + k]
            ids = lab_v[pl.ds(lr, CHUNK), :]
            ob = jnp.sum(jnp.where(mine, occ_b[pl.ds(gb0, CHUNK, stride=n_frames), :], 0.0), axis=1, keepdims=True)
            ol = jnp.sum(jnp.where(mine, occ_l[pl.ds(gb0, CHUNK, stride=n_frames), :], 0.0), axis=1, keepdims=True)
            scale = (ob + ol) / sums[rows, :]
            for j in range(n_grp):
                dz = ex[rows, j * LANES:(j + 1) * LANES] * scale
                if j == 0:
                    dz = dz - jnp.where(lane == 0, ob, 0.0)
                dz = dz - jnp.where(lane + j * LANES == ids, ol, 0.0)
                dz_v[k * CHUNK:(k + 1) * CHUNK, j * LANES:(j + 1) * LANES] = dz.astype(BF16)
        dh_v[...] = dot_nn(dz_v[...], wt_v[...])
        gwo_ref[...] += dot_tn(hid[pl.ds(r0, TILE), :], dz_v[...])
        for k in range(TILE_CHUNKS):
            rows = pl.ds(r0 + k * CHUNK, CHUNK)
            lr = pl.multiple_of(lrow[i * TILE_CHUNKS + k], CHUNK)
            ar = pl.multiple_of(arow[i * TILE_CHUNKS + k] * 8, 8)
            h = hid[rows, :].astype(F32)
            dp = (dh_v[k * CHUNK:(k + 1) * CHUNK, :] * (1.0 - h * h)).astype(BF16).astype(F32)
            dc[pl.ds(lr, CHUNK), :] += dp
            da8[pl.ds(ar, 8), :] += dp[:8, :] + dp[8:, :]
        return carry
    lax.fori_loop(0, n_tiles, bwd_tile, 0)

    n_af = n_utt * n_frames
    d_act_f = jnp.sum(da8[pl.ds(0, n_af * 8), :].reshape(n_af, 8, da8.shape[1]), axis=1).astype(BF16)
    genc_ref[...] = dot_nt(d_act_f, we_v[...]).astype(BF16)
    gwe_ref[...] = dot_tn(f_v[...], d_act_f)
    gwp_ref[...] = dot_tn(g_v[...], dc[pl.ds(0, n_rows), :].astype(BF16))


def local_grads(seq_idx, enc_rows, pred_out, w_enc, w_pred, w_out, labels, frame_len, label_len, n_utt, n_frames, vocab):
    n_pos = labels.shape[1] + 1
    enc_dim, joint = w_enc.shape
    vocab_pad = w_out.shape[1]
    n_rows = n_utt * n_pos
    n_af = n_utt * n_frames
    max_rows = n_utt * n_frames * n_pos
    skew_rows = (n_frames + n_pos) * n_frames
    n_chunks = max_rows // CHUNK + TILE_CHUNKS
    any_spec = pl.BlockSpec(memory_space=pl.ANY)
    vmem = pl.BlockSpec(memory_space=pltpu.VMEM)
    grid_spec = pltpu.PrefetchScalarGridSpec(
        num_scalar_prefetch=3, grid=(),
        in_specs=[any_spec] * 5 + [vmem],
        out_specs=[vmem] * 5,
        scratch_shapes=[
            pltpu.VMEM((n_af, enc_dim), BF16),
            pltpu.VMEM((n_rows, w_pred.shape[0]), BF16),
            pltpu.VMEM(w_enc.shape, BF16),
            pltpu.VMEM(w_pred.shape, BF16),
            pltpu.VMEM(w_out.shape, BF16),
            pltpu.VMEM((vocab_pad, joint), BF16),
            pltpu.VMEM((n_af + 8, joint), F32),
            pltpu.VMEM((n_rows + CHUNK, joint), BF16),
            pltpu.VMEM((n_rows + CHUNK, LANES), jnp.int32),
            pltpu.VMEM((n_utt, LANES), F32),
            pltpu.VMEM((max_rows, joint), BF16),
            pltpu.VMEM((max_rows, vocab_pad), F32),
            pltpu.VMEM((max_rows, LANES), F32),
            pltpu.VMEM((n_utt * skew_rows + 256, LANES), F32),
            pltpu.VMEM((n_utt * skew_rows + 256, LANES), F32),
            pltpu.VMEM((skew_rows, LANES), F32),
            pltpu.VMEM((skew_rows, LANES), F32),
            pltpu.VMEM((skew_rows, LANES), F32),
            pltpu.VMEM((skew_rows + 256, LANES), F32),
            pltpu.VMEM((skew_rows + 256, LANES), F32),
            pltpu.VMEM((TILE, vocab_pad), BF16),
            pltpu.VMEM((TILE, joint), F32),
            pltpu.VMEM((n_rows + CHUNK, joint), F32),
            pltpu.VMEM((n_af * 8 + 8, joint), F32),
            pltpu.SMEM((n_chunks,), jnp.int32),
            pltpu.SMEM((n_chunks,), jnp.int32),
            pltpu.SMEM((n_chunks,), jnp.int32),
            pltpu.SMEM((n_chunks,), jnp.int32),
            pltpu.SMEM((n_chunks,), jnp.int32),
            pltpu.SemaphoreType.DMA((5,)),
        ])
    return pl.pallas_call(
        functools.partial(local_kernel, n_utt, n_frames, n_pos, vocab),
        grid_spec=grid_spec,
        out_shape=[
            jax.ShapeDtypeStruct((8, LANES), F32),
            jax.ShapeDtypeStruct((n_af, enc_dim), BF16),
            jax.ShapeDtypeStruct((enc_dim, joint), F32),
            jax.ShapeDtypeStruct((w_pred.shape[0], joint), F32),
            jax.ShapeDtypeStruct((joint, vocab_pad), F32),
        ],
        compiler_params=pltpu.CompilerParams(vmem_limit_bytes=62 << 20),
        name="rnnt_local",
    )(seq_idx, frame_len, label_len, enc_rows, pred_out, w_enc, w_pred, w_out, labels)


def solution(mesh):
    seq_size = mesh.shape['seq']

    def local_fn(enc_out, pred_out, w_enc, w_pred, w_out, labels, frame_len, label_len):
        seq_idx = lax.axis_index('seq')
        n_all, n_loc, enc_dim = enc_out.shape
        n_utt = n_all // seq_size
        n_frames = n_loc * seq_size
        vocab = w_out.shape[1]
        vocab_pad = pl.cdiv(vocab, LANES) * LANES
        w_out_p = jnp.pad(w_out, ((0, 0), (0, vocab_pad - vocab)))
        enc_mine = lax.all_to_all(enc_out.reshape(seq_size, n_utt, n_loc, enc_dim), 'seq', 0, 0)
        enc_rows = jnp.swapaxes(enc_mine, 0, 1).reshape(n_utt * n_frames, enc_dim)
        loss, genc, gwe, gwp, gwo = local_grads(
            jnp.reshape(seq_idx, (1,)).astype(jnp.int32), enc_rows, pred_out.reshape(-1, pred_out.shape[2]), w_enc, w_pred, w_out_p,
            labels, frame_len, label_len, n_utt, n_frames, vocab)
        genc = jnp.swapaxes(genc.reshape(n_utt, seq_size, n_loc, enc_dim), 0, 1)
        grad_enc = lax.all_to_all(genc, 'seq', 0, 0).reshape(n_all, n_loc, enc_dim)
        gwe, gwp, gwo = lax.psum((gwe, gwp, gwo), 'seq')
        loss = lax.all_gather(loss[0, :n_utt], 'seq').reshape(n_all)
        return loss, grad_enc, gwe, gwp, gwo[:, :vocab]

    in_specs = (P('dp', 'seq', None), P('dp', None, None), P(None, None), P(None, None), P(None, None), P('dp', None), P('dp'), P('dp'))
    out_specs = (P('dp'), P('dp', 'seq', None), P('dp', None), P('dp', None), P('dp', None))
    return jax.shard_map(local_fn, mesh=mesh, in_specs=in_specs, out_specs=out_specs, check_vma=False)
```

time: 429 us -> 163 us (0.38); the launches traced: 424 us -> 163 us
  other arithmetic: 158 us -> 0.66 us
  matrix products: 75 us -> 0 us
  Pallas kernels: 0 us -> 47.8 us
  waiting for transfers between devices: 96.3 us -> 59.6 us
  starting transfers between devices: 36.4 us -> 17.4 us
  local copies, waits for them, and re-layouts: 27.4 us -> 12.9 us
    another operation x64 -> x0, other arithmetic: 116 us -> none  [the longest x16 86.5 us: frame_step(): lax.cumlogsumexp(next_row + frame_blank + lab_sum, axis=1, reverse=True)]
    dot_general x10 -> x0, matrix products: 75 us -> none  [the longest x1 17.6 us: joint_lattice(): jnp.einsum('btuj,buj->btu', hidden, lab_w, preferred_element_type=jnp.flo...]
    pallas_call x0 -> x1, Pallas kernels: none -> 47.8 us  [local_grads(): pl.pallas_call(functools.partial(local_kernel, n_utt, n_frames, n_pos, vo...]
    ppermute x14 -> x0, starting transfers between devices: 36.4 us -> none  [the longest x7 27.2 us: alpha_hop(): received = lax.ppermute(x_out, 'seq', fwd_pairs)]
    ppermute x14 -> x0, waiting for transfers between devices: 34 us -> none  [the longest x7 28.1 us: beta_hop(): received = lax.ppermute(first_row, 'seq', bwd_pairs)]
    all_to_all x0 -> x2, starting transfers between devices: none -> 17.3 us  [the longest x1 13.3 us: local_fn(): grad_enc = lax.all_to_all(genc, 'seq', 0, 0).reshape(n_all, n_loc, enc_dim)]
    psum x1 -> x0, blocking collectives: 15.1 us -> none  [local_fn(): log_prob = lax.psum(jnp.where(seq_idx == 0, first_row[:, 0], 0.0), 'seq')]
    reduce_sum x2 -> x0, other arithmetic: 13.3 us -> none  [the longest x1 9.21 us: joint_backward(): d_act_g = jnp.sum(d_pre, axis=1, dtype=jnp.float32)]
  transfers between devices with their start and end apart: 15 -> 3, of which waited for: 15 -> 2; matrix products, arithmetic and copies ran while one was open for 0% -> 4% of each run, Pallas kernels for 0% -> 0%
where the time goes in v1:
time: 163 us
  waiting for transfers between devices  59.6 us (37%)
  Pallas kernels  47.8 us (29%)
  starting transfers between devices  17.4 us (11%)
  between operations  14.1 us (9%)
  local copies, waits for them, and re-layouts  12.9 us (8%)
  blocking collectives  11.1 us (7%)
    psum x1, waiting for transfers between devices, local_fn(): gwe, gwp, gwo = lax.psum((gwe, gwp, gwo), 'seq')  55.8 us
    pallas_call x1, Pallas kernels, local_grads(): pl.pallas_call(functools.partial(local_kernel, n_utt, n_frames, n_pos, vo...  47.8 us
    all_to_all x1, starting transfers between devices, local_fn(): grad_enc = lax.all_to_all(genc, 'seq', 0, 0).reshape(n_all, n_loc, enc_dim)  13.3 us
    all_gather x1, blocking collectives, local_fn(): loss = lax.all_gather(loss[0, :n_utt], 'seq').reshape(n_all)  11.1 us
    unnamed x8, local copies, waits for them, and re-layouts  8.43 us
    all_to_all x1, starting transfers between devices, local_fn(): lax.all_to_all(enc_out.reshape(seq_size, n_utt, n_loc, enc_dim), 'seq', 0...  4 us
    all_to_all x1, waiting for transfers between devices, local_fn(): lax.all_to_all(enc_out.reshape(seq_size, n_utt, n_loc, enc_dim), 'seq', 0...  3.72 us
  transfers between devices with their start and end apart: 3, of which 2 were waited for; matrix products, arithmetic and copies ran while one was open for 4% of the time, Pallas kernels for 0%

profile of v1, /device:TPU:80, one launch (start us, length us, event | category | flops | bytes accessed | tf_op | source)
XLA Modules:
  0.0 163.5 jit_solution(1242651501273505801)
XLA Ops:
  7.2 4.0 %all-to-all-start = ((bf16[8,8,2,512]{3,2,1,0:T(2,128)(2,1)}), bf16[8,8,2,512]{3,2,1,0:T(2,128)(2,1)S(1)}, u32[]{:S(2)}, u32[]{:S(2)}) async-start(bf16[8,8,2,512]{3,2,1,0:T(2,128)(2,1)} %bitcast.15), calls=%async_computation | async-start | bytes 262144 | tf_op jit(solution)/shard_map/all_to_all | solution.py:302
  11.2 0.1 all-reduce.4.cloned.1.call-start
  11.3 1.2 copy.18
  12.5 0.8 pad.4.wout_hbm
  13.4 3.7 %all-to-all-done = bf16[8,8,2,512]{3,2,1,0:T(2,128)(2,1)S(1)} async-done(((bf16[8,8,2,512]{3,2,1,0:T(2,128)(2,1)}), bf16[8,8,2,512]{3,2,1,0:T(2,128)(2,1)S(1)}, u32[]{:S(2)}, u32[]{:S(2)}) %all-to-all-start) | async-done | bytes 131104 | tf_op jit(solution)/shard_map/all_to_all | solution.py:302
  17.1 0.1 copy.17
  17.2 0.7 reshape.33.enc_hbm
  17.9 47.8 %rnnt_local.1 = (f32[8,128]{1,0:T(8,128)}, bf16[128,512]{1,0:T(8,128)(2,1)}, f32[512,512]{1,0:T(8,128)}, f32[512,512]{1,0:T(8,128)}, f32[512,512]{1,0:T(8,128)}) custom-call(s32[1]{0:T(128)} %bitcast.seq_ref, s32[64]{0:T(128)} %tlen_ref.1, s32[64]{0:T(128)} %ulen_ref.1, bf16[128,512]{1,0:T(8,128)(2,1)} %reshape.33.enc_hbm, bf16[4096,512]{1,0:T(8,128)(2,1)} %bitcast.11, ...), custom_call_target="tpu_custom_call" | custom-call | tf_op jit(solution)/shard_map/rnnt_local/pallas_call | solution.py:276
  65.7 0.1 all-reduce.4.cloned.1.call-update
  65.7 1.0 reshape.36
  66.7 0.8 copy.22
  67.5 13.3 %all-to-all-start.1 = ((bf16[8,8,2,512]{3,2,1,0:T(2,128)(2,1)}), bf16[8,8,2,512]{3,2,1,0:T(2,128)(2,1)S(1)}, u32[]{:S(2)}, u32[]{:S(2)}) async-start(bf16[8,8,2,512]{3,2,1,0:T(2,128)(2,1)} %bitcast.9), calls=%async_computation.1 | async-start | bytes 262144 | tf_op jit(solution)/shard_map/all_to_all | solution.py:308
  80.8 0.7 slice_bitcast_fusion
  81.4 11.1 %all-gather = f32[8,1,8]{2,1,0:T(1,128)S(1)} all-gather(f32[1,1,8]{2,1,0:T(1,128)S(1)} %slice_bitcast_fusion), channel_id=1, replica_groups=mesh['dp'=4,'seq'=8] {'seq'}, dimensions={0}, use_global_device_ids=true | all-gather | bytes 288 | tf_op jit(solution)/shard_map/all_gather | solution.py:310
  92.5 0.5 broadcast.5
  93.0 0.7 reduce.3
  93.7 0.6 reshape.35
  94.3 0.0 all-to-all-done.1
  94.3 55.8 %all-reduce.4.cloned.1.call-done = (f32[512,512]{1,0:T(8,128)}, f32[512,512]{1,0:T(8,128)}, f32[512,512]{1,0:T(8,128)}) async-done(((f32[512,512]{1,0:T(8,128)}, f32[512,512]{1,0:T(8,128)}, f32[512,512]{1,0:T(8,128)}), (f32[512,512]{1,0:T(8,128)}, f32[512,512]{1,0:T(8,128)}, f32[512,512]{1,0:T(8,128)})) %all-reduce.4.cloned.1.call-update) | async-done | bytes 3145744 | tf_op jit(solution)/shard_map/psum | solution.py:309
  150.1 0.0 copy-start
  150.1 2.6 %copy.20 = f32[512,500]{0,1:T(8,128)} copy(f32[512,500]{1,0:T(8,128)} %bitcast.12) | data formatting | bytes 2048000
  152.7 0.7 copy.27
  153.4 2.3 %copy.28 = f32[512,512]{1,0:T(8,128)} copy(f32[512,512]{1,0:T(8,128)} %get-tuple-element.35) | data formatting | bytes 2097152
  155.6 0.0 copy-done
  155.6 1.0 copy.29
Async XLA Ops:
  7.2 9.9 %all-to-all-start = ((bf16[8,8,2,512]{3,2,1,0:T(2,128)(2,1)}), bf16[8,8,2,512]{3,2,1,0:T(2,128)(2,1)S(1)}, u32[]{:S(2)}, u32[]{:S(2)}) async-start(bf16[8,8,2,512]{3,2,1,0:T(2,128)(2,1)} %bitcast.15), calls=%async_computation | async-start | bytes 262144 | tf_op jit(solution)/shard_map/all_to_all | solution.py:302
  11.2 138.9 %all-reduce.4.cloned.1.call-start = ((), (), s32[]{:S(2)}) async-start(), calls=%async_computation.2 | async-start | bytes 6291456 | tf_op jit(solution)/shard_map/psum | solution.py:309
  67.5 26.8 %all-to-all-start.1 = ((bf16[8,8,2,512]{3,2,1,0:T(2,128)(2,1)}), bf16[8,8,2,512]{3,2,1,0:T(2,128)(2,1)S(1)}, u32[]{:S(2)}, u32[]{:S(2)}) async-start(bf16[8,8,2,512]{3,2,1,0:T(2,128)(2,1)} %bitcast.9), calls=%async_computation.1 | async-start | bytes 262144 | tf_op jit(solution)/shard_map/all_to_all | solution.py:308
  150.1 5.5 %copy-start = (f32[512,512]{1,0:T(8,128)S(1)}, f32[512,512]{1,0:T(8,128)}, u32[]{:S(2)}) copy-start(f32[512,512]{1,0:T(8,128)} %get-tuple-element.36) | copy-start | bytes 3145732
Sparse Core Ops, SparseCore 0:
  65.9 84.2 all-reduce.3

commit v2 on v1

--- a/solution.py
+++ b/solution.py
@@ -32,18 +32,18 @@
     return lax.dot_general(x, y, (((1,), (1,)), ((), ())), preferred_element_type=F32)
 
 
-def local_kernel(n_utt, n_frames, n_pos, vocab,
+def local_kernel(n_utt, n_frames, n_loc, n_pos, vocab,
                  seq_ref, tlen_ref, ulen_ref,
-                 enc_hbm, pred_hbm, wenc_hbm, wpred_hbm, wout_hbm, labels_ref,
+                 enc_hbm, pred_hbm, wenc_hbm, wpred_hbm, wout_t_hbm, labels_ref,
                  loss_ref, genc_ref, gwe_ref, gwp_ref, gwo_ref,
-                 f_v, g_v, we_v, wp_v, wo_v, wt_v, act_f, act_g, lab_v, lab_scr,
+                 f_v, g_v, we_v, wp_v, wraw_v, wo_v, wt_v, act_f, act_g, lab_v, lab_scr,
                  hid, ex, sums, sk_b, sk_l, al, xb_s, xl_s, occ_b, occ_l, dz_v, dh_v,
-                 dc, da8, lrow, arow, sbase, gbase, utt_of, sems):
+                 acc_o, dc, da8, lrow, arow, sbase, gbase, utt_of, sems):
     me = seq_ref[0]
     n_diag = n_frames + n_pos - 1
     skew_rows = (n_frames + n_pos) * n_frames
     n_rows = n_utt * n_pos
-    vocab_pad = wo_v.shape[1]
+    vocab_pad = wt_v.shape[0]
     n_grp = vocab_pad // LANES
 
     copies = [
@@ -51,7 +51,7 @@
         pltpu.make_async_copy(pred_hbm.at[pl.ds(pl.multiple_of(me * n_rows, n_rows), n_rows), :], g_v, sems.at[1]),
         pltpu.make_async_copy(wenc_hbm, we_v, sems.at[2]),
         pltpu.make_async_copy(wpred_hbm, wp_v, sems.at[3]),
-        pltpu.make_async_copy(wout_hbm, wo_v, sems.at[4]),
+        pltpu.make_async_copy(wout_t_hbm, wraw_v, sems.at[4]),
     ]
     for cp in copies:
         cp.start()
@@ -63,7 +63,7 @@
         def add_frame(t, pos):
             def add_chunk(q, pos):
                 lrow[pos] = b * n_pos + q * CHUNK
-                arow[pos] = b * n_frames + t
+                arow[pos] = t // n_loc * (n_utt * n_loc) + b * n_loc + t % n_loc
                 skew = (n_frames + 1) * t + n_frames * CHUNK * q
                 sbase[pos] = b * skew_rows + skew
                 gbase[pos] = skew
@@ -86,7 +86,7 @@
 
     dc[...] = jnp.zeros_like(dc)
     da8[...] = jnp.zeros_like(da8)
-    gwo_ref[...] = jnp.zeros_like(gwo_ref)
+    acc_o[...] = jnp.zeros_like(acc_o)
     occ_b[pl.ds(skew_rows, 256), :] = jnp.zeros((256, LANES), F32)
     occ_l[pl.ds(skew_rows, 256), :] = jnp.zeros((256, LANES), F32)
     act_f[pl.ds(n_utt * n_frames, 8), :] = jnp.zeros((8, act_f.shape[1]), F32)
@@ -103,7 +103,9 @@
         cp.wait()
     act_f[pl.ds(0, n_utt * n_frames), :] = dot_nn(f_v[...], we_v[...]).astype(BF16).astype(F32)
     act_g[pl.ds(0, n_rows), :] = dot_nn(g_v[...], wp_v[...]).astype(BF16)
-    wt_v[...] = jnp.transpose(wo_v[...])
+    wt_v[vocab:, :] = jnp.zeros((vocab_pad - vocab, wt_v.shape[1]), BF16)
+    wt_v[:vocab, :] = wraw_v[...]
+    wo_v[...] = jnp.transpose(wt_v[...])
 
     lane = lax.broadcasted_iota(jnp.int32, (CHUNK, LANES), 1)
     last_ok = lane < vocab - (n_grp - 1) * LANES
@@ -207,7 +209,7 @@
                 dz = dz - jnp.where(lane + j * LANES == ids, ol, 0.0)
                 dz_v[k * CHUNK:(k + 1) * CHUNK, j * LANES:(j + 1) * LANES] = dz.astype(BF16)
         dh_v[...] = dot_nn(dz_v[...], wt_v[...])
-        gwo_ref[...] += dot_tn(hid[pl.ds(r0, TILE), :], dz_v[...])
+        acc_o[...] += dot_tn(dz_v[...], hid[pl.ds(r0, TILE), :])
         for k in range(TILE_CHUNKS):
             rows = pl.ds(r0 + k * CHUNK, CHUNK)
             lr = pl.multiple_of(lrow[i * TILE_CHUNKS + k], CHUNK)
@@ -223,13 +225,14 @@
     d_act_f = jnp.sum(da8[pl.ds(0, n_af * 8), :].reshape(n_af, 8, da8.shape[1]), axis=1).astype(BF16)
     genc_ref[...] = dot_nt(d_act_f, we_v[...]).astype(BF16)
     gwe_ref[...] = dot_tn(f_v[...], d_act_f)
+    gwo_ref[...] = acc_o[...]
     gwp_ref[...] = dot_tn(g_v[...], dc[pl.ds(0, n_rows), :].astype(BF16))
 
 
-def local_grads(seq_idx, enc_rows, pred_out, w_enc, w_pred, w_out, labels, frame_len, label_len, n_utt, n_frames, vocab):
+def local_grads(seq_idx, enc_rows, pred_out, w_enc, w_pred, w_out_t, labels, frame_len, label_len, n_utt, n_frames, n_loc, vocab):
     n_pos = labels.shape[1] + 1
     enc_dim, joint = w_enc.shape
-    vocab_pad = w_out.shape[1]
+    vocab_pad = pl.cdiv(vocab, LANES) * LANES
     n_rows = n_utt * n_pos
     n_af = n_utt * n_frames
     max_rows = n_utt * n_frames * n_pos
@@ -246,7 +249,8 @@
             pltpu.VMEM((n_rows, w_pred.shape[0]), BF16),
             pltpu.VMEM(w_enc.shape, BF16),
             pltpu.VMEM(w_pred.shape, BF16),
-            pltpu.VMEM(w_out.shape, BF16),
+            pltpu.VMEM(w_out_t.shape, BF16),
+            pltpu.VMEM((joint, vocab_pad), BF16),
             pltpu.VMEM((vocab_pad, joint), BF16),
             pltpu.VMEM((n_af + 8, joint), F32),
             pltpu.VMEM((n_rows + CHUNK, joint), BF16),
@@ -264,6 +268,7 @@
             pltpu.VMEM((skew_rows + 256, LANES), F32),
             pltpu.VMEM((TILE, vocab_pad), BF16),
             pltpu.VMEM((TILE, joint), F32),
+            pltpu.VMEM((vocab_pad, joint), F32),
             pltpu.VMEM((n_rows + CHUNK, joint), F32),
             pltpu.VMEM((n_af * 8 + 8, joint), F32),
             pltpu.SMEM((n_chunks,), jnp.int32),
@@ -274,18 +279,155 @@
             pltpu.SemaphoreType.DMA((5,)),
         ])
     return pl.pallas_call(
-        functools.partial(local_kernel, n_utt, n_frames, n_pos, vocab),
+        functools.partial(local_kernel, n_utt, n_frames, n_loc, n_pos, vocab),
         grid_spec=grid_spec,
         out_shape=[
             jax.ShapeDtypeStruct((8, LANES), F32),
             jax.ShapeDtypeStruct((n_af, enc_dim), BF16),
             jax.ShapeDtypeStruct((enc_dim, joint), F32),
             jax.ShapeDtypeStruct((w_pred.shape[0], joint), F32),
-            jax.ShapeDtypeStruct((joint, vocab_pad), F32),
+            jax.ShapeDtypeStruct((vocab_pad, joint), F32),
         ],
         compiler_params=pltpu.CompilerParams(vmem_limit_bytes=62 << 20),
         name="rnnt_local",
-    )(seq_idx, frame_len, label_len, enc_rows, pred_out, w_enc, w_pred, w_out, labels)
+    )(seq_idx, frame_len, label_len, enc_rows, pred_out, w_enc, w_pred, w_out_t, labels)
+
+
+def greet(seq_size, me):
+    barrier = pltpu.get_barrier_semaphore()
+    for j in range(1, seq_size):
+        pl.semaphore_signal(barrier, inc=1, device_id={'seq': lax.rem(me + j, seq_size)}, device_id_type=pl.DeviceIdType.MESH)
+    pl.semaphore_wait(barrier, seq_size - 1)
+
+
+def spread_kernel(seq_size, rows, enc_ref, out_ref, send, recv):
+    me = lax.axis_index('seq')
+    greet(seq_size, me)
+    mine = pl.ds(pl.multiple_of(me * rows, rows), rows)
+    copies = []
+    for j in range(1, seq_size):
+        peer = lax.rem(me + j, seq_size)
+        copies.append(pltpu.make_async_remote_copy(
+            src_ref=enc_ref.at[pl.ds(pl.multiple_of(peer * rows, rows), rows), :], dst_ref=out_ref.at[mine, :],
+            send_sem=send.at[j - 1], recv_sem=recv.at[j - 1], device_id={'seq': peer}, device_id_type=pl.DeviceIdType.MESH))
+        copies[-1].start()
+    out_ref[mine, :] = enc_ref[mine, :]
+    for copy in copies:
+        copy.wait()
+
+
+def spread_frames(enc_rows, seq_size):
+    rows = enc_rows.shape[0] // seq_size
+    vmem = pl.BlockSpec(memory_space=pltpu.VMEM)
+    return pl.pallas_call(
+        functools.partial(spread_kernel, seq_size, rows),
+        out_shape=jax.ShapeDtypeStruct(enc_rows.shape, enc_rows.dtype),
+        in_specs=[vmem], out_specs=vmem,
+        scratch_shapes=[pltpu.SemaphoreType.DMA((seq_size - 1,)), pltpu.SemaphoreType.DMA((seq_size - 1,))],
+        compiler_params=pltpu.CompilerParams(collective_id=0, has_side_effects=True),
+        name="spread_frames",
+    )(enc_rows)
+
+
+def reduce_kernel(seq_size, n_mat, genc_ref, loss_ref, *refs):
+    gw = refs[:n_mat]
+    genc_out, loss_out = refs[n_mat:n_mat + 2]
+    out = refs[n_mat + 2:2 * n_mat + 2]
+    rest = refs[2 * n_mat + 2:]
+    sib_buf, own, ring_buf = rest[:n_mat], rest[n_mat:2 * n_mat], rest[2 * n_mat:3 * n_mat]
+    (sib_send, sib_recv, rs_send, rs_recv, ag_send, ag_recv, dd_send, dd_recv,
+     ge_send, ge_recv, lo_send, lo_recv) = rest[3 * n_mat:]
+    me = lax.axis_index('seq')
+    n_chip = seq_size // 2
+    chip, core = lax.div(me, 2), lax.rem(me, 2)
+    sibling = chip * 2 + 1 - core
+    nexts = (lax.rem(chip + 1, n_chip) * 2 + core, lax.rem(chip + n_chip - 1, n_chip) * 2 + core)
+    half = gw[0].shape[0] // 2
+    piece = half // (2 * n_chip)
+
+    def remote(src, dst, send, recv, peer):
+        copy = pltpu.make_async_remote_copy(src_ref=src, dst_ref=dst, send_sem=send, recv_sem=recv,
+                                            device_id={'seq': peer}, device_id_type=pl.DeviceIdType.MESH)
+        copy.start()
+        return copy
+
+    def at(way, hops):
+        c = lax.rem(chip + n_chip - hops, n_chip) if way == 0 else lax.rem(chip + hops, n_chip)
+        return pl.multiple_of((c * 2 + way) * piece, piece)
+
+    greet(seq_size, me)
+    pending = []
+    sib = []
+    for m in range(n_mat):
+        sib.append(remote(gw[m].at[pl.ds(pl.multiple_of((1 - core) * half, half), half), :], sib_buf[m], sib_send.at[m], sib_recv.at[m], sibling))
+    rows = genc_ref.shape[0] // seq_size
+    mine = pl.ds(pl.multiple_of(me * rows, rows), rows)
+    small = []
+    for j in range(1, seq_size):
+        peer = lax.rem(me + j, seq_size)
+        small.append(remote(genc_ref.at[pl.ds(pl.multiple_of(peer * rows, rows), rows), :], genc_out.at[mine, :], ge_send.at[j - 1], ge_recv.at[j - 1], peer))
+        small.append(remote(loss_ref, loss_out.at[me], lo_send.at[j - 1], lo_recv.at[j - 1], peer))
+    genc_out[mine, :] = genc_ref[mine, :]
+    loss_out[pl.ds(me, 1)] = loss_ref[...][None]
+
+    ring = {}
+    for m in range(n_mat):
+        sib[m].wait_recv()
+        own[m][...] = gw[m][pl.ds(pl.multiple_of(core * half, half), half), :] + sib_buf[m][...]
+        for way in range(2):
+            ring[m, way, 0] = remote(own[m].at[pl.ds(at(way, 1), piece), :], ring_buf[m].at[way, 0], rs_send.at[m, way, 0], rs_recv.at[m, way, 0], nexts[way])
+    for s in range(1, n_chip - 1):
+        for m in range(n_mat):
+            for way in range(2):
+                ring[m, way, s - 1].wait_recv()
+                ring_buf[m][way, s - 1] = ring_buf[m][way, s - 1] + own[m][pl.ds(at(way, s + 1), piece), :]
+                ring[m, way, s] = remote(ring_buf[m].at[way, s - 1], ring_buf[m].at[way, s], rs_send.at[m, way, s], rs_recv.at[m, way, s], nexts[way])
+
+    def place(way, hops):
+        return pl.ds(pl.multiple_of(core * half + at(way, hops), piece), piece)
+
+    last = n_chip - 2
+    gather = {}
+    for m in range(n_mat):
+        for way in range(2):
+            ring[m, way, last].wait_recv()
+            here = place(way, 0)
+            out[m][here, :] = ring_buf[m][way, last] + own[m][pl.ds(at(way, 0), piece), :]
+            gather[m, way, 0] = remote(out[m].at[here, :], out[m].at[here, :], ag_send.at[m, way, 0], ag_recv.at[m, way, 0], nexts[way])
+            pending.append(remote(out[m].at[here, :], out[m].at[here, :], dd_send.at[m, way, 0], dd_recv.at[m, way, 0], sibling))
+    for s in range(1, n_chip):
+        for m in range(n_mat):
+            for way in range(2):
+                gather[m, way, s - 1].wait_recv()
+                here = place(way, s)
+                if s < n_chip - 1:
+                    gather[m, way, s] = remote(out[m].at[here, :], out[m].at[here, :], ag_send.at[m, way, s], ag_recv.at[m, way, s], nexts[way])
+                pending.append(remote(out[m].at[here, :], out[m].at[here, :], dd_send.at[m, way, s], dd_recv.at[m, way, s], sibling))
+    for copy in pending + small:
+        copy.wait()
+    for copy in list(ring.values()) + list(gather.values()) + sib:
+        copy.wait_send()
+
+
+def reduce_all(genc, loss, grads, seq_size):
+    n_mat = len(grads)
+    n_chip = seq_size // 2
+    half = grads[0].shape[0] // 2
+    piece = half // (2 * n_chip)
+    vmem = pl.BlockSpec(memory_space=pltpu.VMEM)
+    dma = pltpu.SemaphoreType.DMA
+    steps = n_chip - 1
+    return pl.pallas_call(
+        functools.partial(reduce_kernel, seq_size, n_mat),
+        out_shape=[jax.ShapeDtypeStruct(genc.shape, genc.dtype), jax.ShapeDtypeStruct((seq_size,) + loss.shape, F32)]
+        + [jax.ShapeDtypeStruct(g.shape, F32) for g in grads],
+        in_specs=[vmem] * (2 + n_mat), out_specs=[vmem] * (2 + n_mat),
+        scratch_shapes=[pltpu.VMEM((half, g.shape[1]), F32) for g in grads] * 2
+        + [pltpu.VMEM((2, steps, piece, g.shape[1]), F32) for g in grads]
+        + [dma((n_mat,))] * 2 + [dma((n_mat, 2, steps))] * 4 + [dma((n_mat, 2, n_chip))] * 2 + [dma((seq_size - 1,))] * 4,
+        compiler_params=pltpu.CompilerParams(collective_id=1, has_side_effects=True),
+        name="reduce_all",
+    )(genc, loss, *grads)
 
 
 def solution(mesh):
@@ -297,18 +439,12 @@
         n_utt = n_all // seq_size
         n_frames = n_loc * seq_size
         vocab = w_out.shape[1]
-        vocab_pad = pl.cdiv(vocab, LANES) * LANES
-        w_out_p = jnp.pad(w_out, ((0, 0), (0, vocab_pad - vocab)))
-        enc_mine = lax.all_to_all(enc_out.reshape(seq_size, n_utt, n_loc, enc_dim), 'seq', 0, 0)
-        enc_rows = jnp.swapaxes(enc_mine, 0, 1).reshape(n_utt * n_frames, enc_dim)
-        loss, genc, gwe, gwp, gwo = local_grads(
-            jnp.reshape(seq_idx, (1,)).astype(jnp.int32), enc_rows, pred_out.reshape(-1, pred_out.shape[2]), w_enc, w_pred, w_out_p,
-            labels, frame_len, label_len, n_utt, n_frames, vocab)
-        genc = jnp.swapaxes(genc.reshape(n_utt, seq_size, n_loc, enc_dim), 0, 1)
-        grad_enc = lax.all_to_all(genc, 'seq', 0, 0).reshape(n_all, n_loc, enc_dim)
-        gwe, gwp, gwo = lax.psum((gwe, gwp, gwo), 'seq')
-        loss = lax.all_gather(loss[0, :n_utt], 'seq').reshape(n_all)
-        return loss, grad_enc, gwe, gwp, gwo[:, :vocab]
+        enc_rows = spread_frames(enc_out.reshape(n_all * n_loc, enc_dim), seq_size)
+        loss, genc, *grads = local_grads(
+            jnp.reshape(seq_idx, (1,)).astype(jnp.int32), enc_rows, pred_out.reshape(-1, pred_out.shape[2]), w_enc, w_pred, w_out.T,
+            labels, frame_len, label_len, n_utt, n_frames, n_loc, vocab)
+        genc, loss, gwe, gwp, gwo_t = reduce_all(genc, loss, grads, seq_size)
+        return loss[:, 0, :n_utt].reshape(n_all), genc.reshape(n_all, n_loc, enc_dim), gwe, gwp, gwo_t[:vocab].T
 
     in_specs = (P('dp', 'seq', None), P('dp', None, None), P(None, None), P(None, None), P(None, None), P('dp', None), P('dp'), P('dp'))
     out_specs = (P('dp'), P('dp', 'seq', None), P('dp', None), P('dp', None), P('dp', None))

time: 163 us -> 123 us (0.75)
  the two profiles are of different devices: /device:TPU:80 before, /device:TPU:89 now
where the time goes in v2:
time: 123 us; the launch traced here: 124 us
  Pallas kernels  113 us (92%)
  local copies, waits for them, and re-layouts  10.2 us (8%)
    pallas_call x1, Pallas kernels, local_grads(): pl.pallas_call(functools.partial(local_kernel, n_utt, n_frames, n_loc, n_...  63.9 us
    pallas_call x1, Pallas kernels, reduce_all(): pl.pallas_call(functools.partial(reduce_kernel, seq_size, n_mat), out_sha...  40.1 us
    pallas_call x1, Pallas kernels, spread_frames(): pl.pallas_call(functools.partial(spread_kernel, seq_size, rows), out_shap...  8.72 us
    unnamed x4, local copies, waits for them, and re-layouts  3.24 us

profile of v2, /device:TPU:89, one launch (start us, length us, event | category | flops | bytes accessed | tf_op | source)
XLA Modules:
  0.0 123.6 jit_solution(14999922332625109766)
XLA Ops:
  0.6 1.6 %reshape.23.enc_ref = bf16[128,512]{1,0:T(8,128)(2,1)} reshape(bf16[64,2,512]{2,1,0:T(2,128)(2,1)} %param.8) | data formatting | bytes 262144 | tf_op jit(solution)/shard_map/reshape | solution.py:442
  2.3 8.7 %spread_frames.1.enc_hbm = bf16[128,512]{1,0:T(8,128)(2,1)} custom-call(bf16[128,512]{1,0:T(8,128)(2,1)} %reshape.23.enc_ref), custom_call_target="tpu_custom_call" | custom-call | tf_op jit(solution)/shard_map/spread_frames/pallas_call | solution.py:322
  11.0 63.9 %rnnt_local.1 = (f32[8,128]{1,0:T(8,128)}, bf16[128,512]{1,0:T(8,128)(2,1)}, f32[512,512]{1,0:T(8,128)}, f32[512,512]{1,0:T(8,128)}, f32[512,512]{1,0:T(8,128)}) custom-call(s32[1]{0:T(128)} %bitcast.seq_ref, s32[64]{0:T(128)} %tlen_ref.1, s32[64]{0:T(128)} %ulen_ref.1, bf16[128,512]{1,0:T(8,128)(2,1)} %spread_frames.1.enc_hbm, bf16[4096,512]{1,0:T(8,128)(2,1)} %bitcast.5, ...), custom_call_target="tpu_custom_call" | custom-call | tf_op jit(solution)/shard_map/rnnt_local/pallas_call | solution.py:281
  74.9 40.1 %reduce_all.1 = (bf16[128,512]{1,0:T(8,128)(2,1)}, f32[8,8,128]{2,1,0:T(8,128)}, f32[512,512]{1,0:T(8,128)}, f32[512,512]{1,0:T(8,128)}, f32[512,512]{1,0:T(8,128)}) custom-call(bf16[128,512]{1,0:T(8,128)(2,1)} %get-tuple-element.15.genc_ref, f32[8,128]{1,0:T(8,128)} %get-tuple-element.16.loss_ref, f32[512,512]{1,0:T(8,128)} %get-tuple-element.17.refs_0_, ...), custom_call_target="tpu_custom_call" | custom-call | tf_op jit(solution)/shard_map/reduce_all/pallas_call | solution.py:420
  115.0 0.0 copy-start
  115.0 0.9 slice_reduce_fusion
  115.9 0.6 reshape_squeeze.3
  116.5 1.6 %reshape.25 = bf16[64,2,512]{2,1,0:T(2,128)(2,1)} reshape(bf16[128,512]{1,0:T(8,128)(2,1)} %get-tuple-element.21) | data formatting | bytes 262144 | tf_op jit(solution)/shard_map/reshape | solution.py:447
  118.1 2.2 %slice_bitcast_fusion = f32[512,500]{0,1:T(8,128)} fusion(f32[512,512]{1,0:T(8,128)} %get-tuple-element.24), kind=kLoop, calls=%fused_computation | loop fusion | bytes 2048000 | tf_op jit(solution)/shard_map/transpose | solution.py:447
  120.4 2.3 %copy.15 = f32[512,512]{1,0:T(8,128)} copy(f32[512,512]{1,0:T(8,128)} %get-tuple-element.32) | data formatting | bytes 2097152
  122.6 0.0 copy-done
  122.6 1.0 copy.16
Async XLA Ops:
  115.0 7.6 %copy-start = (f32[512,512]{1,0:T(8,128)S(1)}, f32[512,512]{1,0:T(8,128)}, u32[]{:S(2)}) copy-start(f32[512,512]{1,0:T(8,128)} %get-tuple-element.33) | copy-start | bytes 3145732
